TPU v7x, 32 devices: a whole 2x2x4 slice. The times are simulated.
32 devices in a mesh: aux: 4 (over y, x), pair: 8 (over z, core).
Axes of the slice: x: 2, y: 2, z: 4, core: 2. Of those that a mesh axis runs over, the one named last changes fastest.
Arguments:
- m_panels: bfloat16 [40000, 8192], P('aux', 'pair'), may hold values from -6 to 6
- lower_cols: bfloat16 [2, 512, 40000], P(None, 'pair', 'aux'), may hold values from -0.2 to 0.2, as said below
- diag_inverses: float32 [2, 512, 512], replicated, may hold values from -0.2 to 2, as said below
Outputs:
- remainder: bfloat16 [40000, 8192], P('aux', 'pair')
- solved: bfloat16 [2, 512, 8192], P(None, None, 'pair')
Inputs may be any that keep to these rules, and one draw needn't show every extreme that they name: lower_cols[k] is zero in the pivot rows of panels 0 to k (the factor is lower triangular and its diagonal blocks are given by their inverses). Each diag_inverses[k] is lower triangular.
All inputs are finite; a program needn't handle non-finite values.
Results may differ from a plain program's by a relative error of at most 0.0047.
Values may be sent and summed in bfloat16 or wider, within the bound.
A program may use at most 192 MiB of HBM per device.

v0:
```python
import jax
import jax.numpy as jnp
from jax import lax
from jax.sharding import PartitionSpec as P


def spread(block, axis, source):
    block = jnp.where(lax.axis_index(axis) == source, block, jnp.zeros_like(block))
    return lax.psum(block, axis)


def settle(panel, pivot, diag_inverses):
    local = jnp.dot(
        diag_inverses[panel],
        pivot,
        precision=lax.Precision.HIGHEST,
        preferred_element_type=jnp.float32,
    ).astype(jnp.bfloat16)
    return spread(local, "aux", panel)


def shards(m_panels, lower_cols, diag_inverses):
    panels = diag_inverses.shape[0]
    width = diag_inverses.shape[1]
    work = m_panels.astype(jnp.float32)
    results = []
    for panel in range(panels):
        solved_rows = settle(panel, work[:width], diag_inverses)

        def subtract(carry, piece, start, solved_rows=solved_rows):
            return carry - lax.dot_general(
                piece, solved_rows, (((0,), (0,)), ((), ())), preferred_element_type=jnp.float32
            )

        work = subtract(
            work, lax.all_gather(lower_cols[panel], "pair", axis=0, tiled=True), jnp.int32(0)
        )
        results.append(solved_rows)
    return (work.astype(jnp.bfloat16), jnp.stack(results))


def solution(mesh):
    placed = (P("aux", "pair"), P(None, "pair", "aux"), P())
    return jax.shard_map(
        shards,
        mesh=mesh,
        in_specs=placed,
        out_specs=(P("aux", "pair"), P(None, None, "pair")),
        check_vma=False,
    )
```

profile of v0, /device:TPU:0, one launch (start us, length us, event | category | flops | bytes accessed | tf_op | source)
XLA Modules:
  0.0 282.0 jit_solution(16829166616042446684)
XLA Ops:
  8.0 0.0 all-reduce.3.cloned.1.call-start
  8.0 4.3 %fusion.8 = bf16[512,1024]{1,0:T(8,128)(2,1)} fusion(bf16[10000,1024]{1,0:T(8,128)(2,1)} %param.3, f32[2,512,512]{2,1,0:T(8,128)} %param.5, pred[]{:T(512)S(6)} %eq.6), kind=kOutput, calls=%fused_computation.10 | convolution fusion | flops 3222274048 | bytes 3145729 | tf_op jit(solution)/shard_map/dot_general | solution.py:13
  12.4 0.0 all-reduce.3.cloned.1.call-update
  12.4 0.0 all-gather.5.cloned.1.call-start
  12.4 3.3 %fusion.20 = (bf16[1,64,10000]{2,1,0:T(8,128)(2,1)}, bf16[1,64,10000]{2,1,0:T(8,128)(2,1)}) fusion(bf16[2,64,10000]{2,1,0:T(8,128)(2,1)} %param.4), kind=kLoop, calls=%fused_computation.18 | loop fusion | bytes 5120000 | tf_op jit(solution)/shard_map/slice | solution.py:36
  15.8 0.0 all-gather.5.cloned.1.call-update
  15.8 0.0 all-reduce.5.cloned.1.call-start
  15.9 0.0 copy-start.1
  15.9 51.9 %all-reduce.3.cloned.1.call-done = bf16[512,1024]{1,0:T(8,128)(2,1)} async-done(((bf16[512,1024]{1,0:T(8,128)(2,1)}), bf16[512,1024]{1,0:T(8,128)(2,1)}) %all-reduce.3.cloned.1.call-update) | async-done | bytes 1048592 | tf_op jit(solution)/shard_map/psum | solution.py:9
  67.7 0.0 copy-start
  67.7 49.1 %all-gather.5.cloned.1.call-done = bf16[1,512,10000]{2,1,0:T(8,128)(2,1)} async-done(((bf16[1,64,10000]{2,1,0:T(8,128)(2,1)}), bf16[1,512,10000]{2,1,0:T(8,128)(2,1)}) %all-gather.5.cloned.1.call-update) | async-done | bytes 10240016 | tf_op jit(solution)/shard_map/all_gather | solution.py:36
  116.8 27.4 %bitcast_subtract_fusion.1 = f32[10000,1024]{1,0:T(8,128)} fusion(bf16[10000,1024]{1,0:T(8,128)(2,1)} %param.3, bf16[512,1024]{1,0:T(8,128)(2,1)} %all-reduce.3.cloned.1.call-done, bf16[1,512,10000]{2,1,0:T(8,128)(2,1)} %all-gather.5.cloned.1.call-done), kind=kOutput, calls=%fused_computation.2 | convolution fusion | flops 10506240000 | bytes 72728576 | tf_op jit(solution)/shard_map/dot_general | solution.py:31
  144.2 0.0 copy-done.1
  144.2 6.1 %fusion.12 = bf16[512,1024]{1,0:T(8,128)(2,1)} fusion(f32[10000,1024]{1,0:T(8,128)} %bitcast_subtract_fusion.1, f32[2,512,512]{2,1,0:T(8,128)S(1)} %copy-done.1, pred[]{:T(512)S(6)} %eq.7), kind=kOutput, calls=%fused_computation.12 | convolution fusion | flops 3222274048 | bytes 4194305 | tf_op jit(solution)/shard_map/dot_general | solution.py:13
  150.3 0.0 all-reduce.5.cloned.1.call-update
  150.3 0.2 all-gather.7.cloned.1.call-start
  150.5 0.4 all-gather.7.cloned.1.call-update
  150.9 50.4 %all-reduce.5.cloned.1.call-done = bf16[512,1024]{1,0:T(8,128)(2,1)} async-done(((bf16[512,1024]{1,0:T(8,128)(2,1)}), bf16[512,1024]{1,0:T(8,128)(2,1)}) %all-reduce.5.cloned.1.call-update) | async-done | bytes 1048592 | tf_op jit(solution)/shard_map/psum | solution.py:9
  201.2 0.0 copy-done
  201.2 2.7 pad_maximum_fusion
  204.0 45.5 %all-gather.7.cloned.1.call-done = bf16[1,512,10000]{2,1,0:T(8,128)(2,1)} async-done(((bf16[1,64,10000]{2,1,0:T(8,128)(2,1)}), bf16[1,512,10000]{2,1,0:T(8,128)(2,1)}) %all-gather.7.cloned.1.call-update) | async-done | bytes 10240016 | tf_op jit(solution)/shard_map/all_gather | solution.py:36
  249.5 25.0 %fusion = bf16[10000,1024]{1,0:T(8,128)(2,1)} fusion(f32[10000,1024]{1,0:T(8,128)} %bitcast_subtract_fusion.1, bf16[512,1024]{1,0:T(8,128)(2,1)} %all-reduce.5.cloned.1.call-done, bf16[1,512,10000]{2,1,0:T(8,128)(2,1)} %all-gather.7.cloned.1.call-done), kind=kOutput, calls=%fused_computation.1 | convolution fusion | flops 10506240000 | bytes 72728576 | tf_op jit(solution)/shard_map/dot_general | solution.py:31
Async XLA Ops:
  8.0 59.7 %all-reduce.3.cloned.1.call-start = ((), (), s32[]{:S(2)}) async-start(), calls=%async_computation | async-start | bytes 2097152 | tf_op jit(solution)/shard_map/psum | solution.py:9
  12.4 104.4 %all-gather.5.cloned.1.call-start = ((), (), s32[]{:S(2)}) async-start(), calls=%async_computation.2 | async-start | bytes 11649024 | tf_op jit(solution)/shard_map/all_gather | solution.py:36
  15.8 185.4 %all-reduce.5.cloned.1.call-start = ((), (), s32[]{:S(2)}) async-start(), calls=%async_computation.1 | async-start | bytes 2097152 | tf_op jit(solution)/shard_map/psum | solution.py:9
  15.9 128.3 %copy-start.1 = (f32[2,512,512]{2,1,0:T(8,128)S(1)}, f32[2,512,512]{2,1,0:T(8,128)}, u32[]{:S(2)}) copy-start(f32[2,512,512]{2,1,0:T(8,128)} %param.5) | copy-start | bytes 6291460
  67.7 133.5 %copy-start = (bf16[512,1024]{1,0:T(8,128)(2,1)S(1)}, bf16[512,1024]{1,0:T(8,128)(2,1)}, u32[]{:S(2)}) copy-start(bf16[512,1024]{1,0:T(8,128)(2,1)} %all-reduce.3.cloned.1.call-done) | copy-start | bytes 3145732
  150.3 99.2 %all-gather.7.cloned.1.call-start = ((), (), s32[]{:S(2)}) async-start(), calls=%async_computation.3 | async-start | bytes 11649024 | tf_op jit(solution)/shard_map/all_gather | solution.py:36
Sparse Core Ops, SparseCore 0:
  12.5 55.1 all-reduce.2
  150.4 50.7 all-reduce.4
Sparse Core Ops, SparseCore 1:
  15.9 100.9 all-gather.4
  153.0 96.5 all-gather.6
where the time goes:
time: 282 us
  waiting for transfers between devices  197 us (70%)
  matrix products  62.8 us (22%)
  between operations  15.5 us (5%)
  local copies, waits for them, and re-layouts  3.36 us (1%)
    psum x2, waiting for transfers between devices, spread(): return lax.psum(block, axis)  102 us
    all_gather x2, waiting for transfers between devices, shards(): lax.all_gather(lower_cols[panel], 'pair', axis=0, tiled=True)  94.6 us
    dot_general x2, matrix products, subtract(): lax.dot_general(piece, solved_rows, (((0,), (0,)), ((), ())), preferred_e...  52.4 us
    dot_general x2, matrix products, settle(): jnp.dot(diag_inverses[panel], pivot, precision=lax.Precision.HIGHEST, pre...  10.4 us
  transfers between devices with their start and end apart: 4, of which 4 were waited for; matrix products, arithmetic and copies ran while one was open for 2% of the time, Pallas kernels for 0%

commit v1 on v0

--- a/solution.py
+++ b/solution.py
@@ -6,7 +6,7 @@
 
 def spread(block, axis, source):
     block = jnp.where(lax.axis_index(axis) == source, block, jnp.zeros_like(block))
-    return lax.psum(block, axis)
+    return jnp.sum(lax.all_gather(block, axis), axis=0)
 
 
 def settle(panel, pivot, diag_inverses):

time: 282 us -> 389 us (1.38)
  waiting for transfers between devices: 197 us -> 282 us
  other arithmetic: 2.75 us -> 12.6 us
  local copies, waits for them, and re-layouts: 3.36 us -> 11.7 us
  matrix products: 62.8 us -> 67.9 us
    psum x2 -> x0, waiting for transfers between devices: 102 us -> none  [spread(): return lax.psum(block, axis)]
    all_gather x0 -> x2, waiting for transfers between devices: none -> 102 us  [spread(): return jnp.sum(lax.all_gather(block, axis), axis=0)]
    all_gather x2, waiting for transfers between devices: 94.6 us -> 179 us  [shards(): lax.all_gather(lower_cols[panel], 'pair', axis=0, tiled=True)]
    reduce_sum x0 -> x2, other arithmetic: none -> 11.1 us  [spread(): return jnp.sum(lax.all_gather(block, axis), axis=0)]
    all_gather x0 -> x1, local copies, waits for them, and re-layouts: none -> 7.81 us  [spread(): return jnp.sum(lax.all_gather(block, axis), axis=0)]
  transfers between devices with their start and end apart: 4 -> 4, of which waited for: 4 -> 4; matrix products, arithmetic and copies ran while one was open for 2% -> 6% of each run, Pallas kernels for 0% -> 0%
where the time goes in v1:
time: 389 us; the launch traced here: 388 us
  waiting for transfers between devices  282 us (72%)
  matrix products  67.9 us (17%)
  between operations  13.8 us (4%)
  other arithmetic  12.6 us (3%)
  local copies, waits for them, and re-layouts  11.7 us (3%)
    all_gather x2, waiting for transfers between devices, shards(): lax.all_gather(lower_cols[panel], 'pair', axis=0, tiled=True)  179 us
    all_gather x2, waiting for transfers between devices, spread(): return jnp.sum(lax.all_gather(block, axis), axis=0)  102 us
    dot_general x2, matrix products, subtract(): lax.dot_general(piece, solved_rows, (((0,), (0,)), ((), ())), preferred_e...  54.3 us
    dot_general x2, matrix products, settle(): jnp.dot(diag_inverses[panel], pivot, precision=lax.Precision.HIGHEST, pre...  13.5 us
    reduce_sum x2, other arithmetic, spread(): return jnp.sum(lax.all_gather(block, axis), axis=0)  11.1 us
    all_gather x1, local copies, waits for them, and re-layouts, spread(): return jnp.sum(lax.all_gather(block, axis), axis=0)  7.81 us
  transfers between devices with their start and end apart: 4, of which 4 were waited for; matrix products, arithmetic and copies ran while one was open for 6% of the time, Pallas kernels for 0%

profile of v1, /device:TPU:0, one launch (start us, length us, event | category | flops | bytes accessed | tf_op | source)
XLA Modules:
  0.0 388.4 jit_solution(15374526618500499829)
XLA Ops:
  7.2 0.0 all-gather.9.cloned.1.call-start
  7.2 4.3 %fusion.8 = bf16[512,1024]{1,0:T(8,128)(2,1)} fusion(bf16[10000,1024]{1,0:T(8,128)(2,1)} %param.3, f32[2,512,512]{2,1,0:T(8,128)} %param.5, pred[]{:T(512)S(6)} %eq.6), kind=kOutput, calls=%fused_computation.10 | convolution fusion | flops 3222274048 | bytes 3145729 | tf_op jit(solution)/shard_map/dot_general | solution.py:13
  11.5 0.0 all-gather.9.cloned.1.call-update
  11.6 0.0 all-gather.11.cloned.1.call-start
  11.6 3.3 fusion.20
  15.0 0.0 all-gather.11.cloned.1.call-update
  15.0 0.2 all-gather.13.cloned.1.call-start
  15.2 51.8 %all-gather.9.cloned.1.call-done = bf16[2048,1024]{1,0:T(8,128)(2,1)} async-done(((bf16[512,1024]{1,0:T(8,128)(2,1)}), bf16[2048,1024]{1,0:T(8,128)(2,1)}) %all-gather.9.cloned.1.call-update) | async-done | bytes 4194320 | tf_op jit(solution)/shard_map/all_gather | solution.py:9
  67.0 3.3 reduce_sum.24
  70.3 0.0 copy-start
  70.3 97.2 %all-gather.11.cloned.1.call-done = bf16[1,512,10000]{2,1,0:T(8,128)(2,1)} async-done(((bf16[1,64,10000]{2,1,0:T(8,128)(2,1)}), bf16[1,512,10000]{2,1,0:T(8,128)(2,1)}) %all-gather.11.cloned.1.call-update) | async-done | bytes 10240016 | tf_op jit(solution)/shard_map/all_gather | solution.py:36
  167.5 29.5 %bitcast_subtract_fusion.1 = f32[10000,1024]{1,0:T(8,128)} fusion(bf16[10000,1024]{1,0:T(8,128)(2,1)} %param.3, bf16[512,1024]{1,0:T(8,128)(2,1)S(1)} %reduce_sum.24, bf16[1,512,10000]{2,1,0:T(8,128)(2,1)} %all-gather.11.cloned.1.call-done), kind=kOutput, calls=%fused_computation.2 | convolution fusion | flops 10506240000 | bytes 72728576 | tf_op jit(solution)/shard_map/dot_general | solution.py:31
  197.1 0.0 copy-done
  197.1 9.2 %fusion.12 = bf16[512,1024]{0,1:T(8,128)(2,1)} fusion(f32[10000,1024]{1,0:T(8,128)} %bitcast_subtract_fusion.1, f32[2,512,512]{2,1,0:T(8,128)S(1)} %copy-done, pred[]{:T(512)S(6)} %eq.7), kind=kOutput, calls=%fused_computation.12 | convolution fusion | flops 3222274048 | bytes 4194305 | tf_op jit(solution)/shard_map/dot_general | solution.py:13
  206.3 0.0 all-gather.13.cloned.1.call-update
  206.3 0.3 all-gather.15.cloned.1.call-start
  206.6 0.3 all-gather.15.cloned.1.call-update
  206.9 50.4 %all-gather.13.cloned.1.call-done = bf16[2048,1024]{0,1:T(8,128)(2,1)} async-done(((bf16[512,1024]{0,1:T(8,128)(2,1)}), bf16[2048,1024]{0,1:T(8,128)(2,1)}) %all-gather.13.cloned.1.call-update) | async-done | bytes 4194320 | tf_op jit(solution)/shard_map/all_gather | solution.py:9
  257.3 7.8 %reshape.6 = bf16[4,512,1024]{1,0,2:T(4,128)(2,1)} reshape(bf16[2048,1024]{0,1:T(8,128)(2,1)} %all-gather.13.cloned.1.call-done) | data formatting | bytes 8388608 | tf_op jit(solution)/shard_map/all_gather | solution.py:9
  265.1 7.8 %reduce_sum.25 = bf16[512,1024]{0,1:T(8,128)(2,1)S(1)} reduce(bf16[4,512,1024]{1,0,2:T(4,128)(2,1)} %reshape.6, bf16[]{:T(256)} %constant.12.clone.1), dimensions={0}, to_apply=%region_1.2 | reduce | flops 1572864 | bytes 5242882 | tf_op jit(solution)/shard_map/reduce_sum | solution.py:9
  272.9 0.5 copy.6
  273.4 1.5 pad_maximum_fusion
  274.9 82.2 %all-gather.15.cloned.1.call-done = bf16[1,512,10000]{2,1,0:T(8,128)(2,1)} async-done(((bf16[1,64,10000]{2,1,0:T(8,128)(2,1)}), bf16[1,512,10000]{2,1,0:T(8,128)(2,1)}) %all-gather.15.cloned.1.call-update) | async-done | bytes 10240016 | tf_op jit(solution)/shard_map/all_gather | solution.py:36
  357.1 24.8 %fusion = bf16[10000,1024]{1,0:T(8,128)(2,1)} fusion(f32[10000,1024]{1,0:T(8,128)} %bitcast_subtract_fusion.1, bf16[512,1024]{0,1:T(8,128)(2,1)S(1)} %reduce_sum.25, bf16[1,512,10000]{2,1,0:T(8,128)(2,1)} %all-gather.15.cloned.1.call-done), kind=kOutput, calls=%fused_computation.1 | convolution fusion | flops 10506240000 | bytes 72728576 | tf_op jit(solution)/shard_map/dot_general | solution.py:31
Async XLA Ops:
  7.2 59.8 %all-gather.9.cloned.1.call-start = ((), (), s32[]{:S(2)}) async-start(), calls=%async_computation | async-start | bytes 5242880 | tf_op jit(solution)/shard_map/all_gather | solution.py:9
  11.6 156.0 %all-gather.11.cloned.1.call-start = ((), (), s32[]{:S(2)}) async-start(), calls=%async_computation.1 | async-start | bytes 11649024 | tf_op jit(solution)/shard_map/all_gather | solution.py:36
  15.0 242.3 %all-gather.13.cloned.1.call-start = ((), (), s32[]{:S(2)}) async-start(), calls=%async_computation.2 | async-start | bytes 5242880 | tf_op jit(solution)/shard_map/all_gather | solution.py:9
  70.3 126.8 %copy-start = (f32[2,512,512]{2,1,0:T(8,128)S(1)}, f32[2,512,512]{2,1,0:T(8,128)}, u32[]{:S(2)}) copy-start(f32[2,512,512]{2,1,0:T(8,128)} %param.5) | copy-start | bytes 6291460
  206.3 150.8 %all-gather.15.cloned.1.call-start = ((), (), s32[]{:S(2)}) async-start(), calls=%async_computation.3 | async-start | bytes 11649024 | tf_op jit(solution)/shard_map/all_gather | solution.py:36
Sparse Core Ops, SparseCore 0:
  11.7 55.2 all-gather.8
  69.2 98.2 all-gather.10
  206.5 50.7 all-gather.12
  258.8 98.2 all-gather.14
